TPU v7x, 32 devices: a whole 2x2x4 slice. The times are simulated.
32 devices in a mesh: grp: 1, win: 32 (over z, y, x, core).
Axes of the slice: x: 2, y: 2, z: 4, core: 2. Of those that a mesh axis runs over, the one named last changes fastest.
Arguments:
- tokens: bfloat16 [2, 8, 64, 96, 384], P('grp', None, None, 'win'), may hold values from -6 to 6
- w_upper: bfloat16 [384, 640], replicated, may hold values from -0.3125 to 0.3125
- w_surface: bfloat16 [384, 256], replicated, may hold values from -0.3125 to 0.3125
- bias: float32 [69], replicated, may hold values from -1 to 1
Outputs:
- fields: bfloat16 [2, 17664, 384], P('grp', 'win')
All inputs are finite; a program needn't handle non-finite values.
Results may differ from a plain program's by a relative error of at most 0.0048.
Values may be sent and summed in bfloat16 or wider, within the bound.
A program may use at most 128 MiB of HBM per device.

v0:
```python
import jax
import jax.numpy as jnp
from jax import lax
from jax.sharding import PartitionSpec as P

VARS_UP = 5
LEVELS = 13
VARS_SF = 4
PATCH = 4


def intersection_add(values, axis):
    first = lax.index_in_dim(values, 0, axis + 1, keepdims=False)
    second = lax.index_in_dim(values, 1, axis + 1, keepdims=False)
    pad_first = [(0, 0)] * first.ndim
    pad_second = [(0, 0)] * first.ndim
    pad_first[axis] = (0, 1)
    pad_second[axis] = (1, 0)
    return jnp.pad(first, pad_first) + jnp.pad(second, pad_second)


def latitude_add(values):
    first = values[..., 0, :, :]
    second = values[..., 1, :, :]
    pad_first = [(0, 0)] * (first.ndim - 1) + [(0, 1)]
    pad_second = [(0, 0)] * (first.ndim - 1) + [(1, 0)]
    summed = jnp.pad(first, pad_first) + jnp.pad(second, pad_second)
    return jnp.swapaxes(summed, -1, -2)


def project(tokens, w_upper, w_surface):
    members, tok_levels, lat_rows, lon_cols, width = tokens.shape
    upper_levels = tok_levels - 1
    rim_width = PATCH // 2
    frame_width = (lon_cols + 1) * PATCH
    upper_tok = jnp.transpose(tokens[:, :upper_levels], (0, 1, 3, 4, 2))
    kernel_up = w_upper.reshape(width, VARS_UP, 2, 2, PATCH, 2, PATCH)
    upper = jnp.einsum(
        "dvlpqrs,mzjdi->vlpqrsmzji", kernel_up, upper_tok, preferred_element_type=jnp.float32
    )
    upper = jnp.transpose(upper, (6, 8, 4, 5, 0, 7, 1, 2, 3, 9))
    upper = intersection_add(upper, 1)
    upper = latitude_add(upper)
    upper = upper.reshape(members, frame_width, VARS_UP, 2 * upper_levels, (lat_rows + 1) * PATCH)
    upper = upper[:, :, :, :LEVELS, rim_width : rim_width + lat_rows * PATCH]
    upper = upper.reshape(members, frame_width, VARS_UP * LEVELS, lat_rows * PATCH)
    surface_tok = jnp.transpose(tokens[:, upper_levels], (0, 2, 3, 1))
    kernel_sf = w_surface.reshape(width, VARS_SF, 2, PATCH, 2, PATCH)
    surface = jnp.einsum(
        "dvpqrs,mjdi->vpqrsmji", kernel_sf, surface_tok, preferred_element_type=jnp.float32
    )
    surface = jnp.transpose(surface, (5, 6, 3, 4, 0, 1, 2, 7))
    surface = intersection_add(surface, 1)
    surface = latitude_add(surface)
    surface = surface.reshape(members, frame_width, VARS_SF, (lat_rows + 1) * PATCH)
    surface = surface[:, :, :, rim_width : rim_width + lat_rows * PATCH]
    joined = jnp.concatenate([upper, surface], axis=2).astype(jnp.bfloat16)
    return joined.reshape(members, frame_width, -1)


def deliver(frames, bias, lat_rows):
    rim_width = PATCH // 2
    members, frame_width, all_rows = frames.shape
    columns = frame_width - 2 * rim_width
    windows = lax.axis_size("win")
    received = lax.all_to_all(frames, "win", split_axis=2, concat_axis=1, tiled=True)
    own_rows = received.shape[2]
    received = received.reshape(members, windows, frame_width, own_rows)
    inner = received[:, :, rim_width : frame_width - rim_width, :].astype(jnp.float32)
    from_left = jnp.roll(received[:, :, frame_width - rim_width :, :], 1, axis=1).astype(
        jnp.float32
    )
    from_right = jnp.roll(received[:, :, :rim_width, :], -1, axis=1).astype(jnp.float32)
    summed = inner + jnp.pad(from_left, ((0, 0), (0, 0), (0, columns - rim_width), (0, 0)))
    summed = summed + jnp.pad(from_right, ((0, 0), (0, 0), (columns - rim_width, 0), (0, 0)))
    first_row = lax.axis_index("win") * own_rows
    row_ids = first_row + jnp.arange(own_rows, dtype=jnp.int32)
    channel = row_ids // (lat_rows * PATCH)
    selector = (channel[:, None] == jnp.arange(bias.shape[0], dtype=jnp.int32)[None, :]).astype(
        jnp.float32
    )
    bias_rows = jnp.dot(selector, bias, precision=lax.Precision.HIGHEST)
    image = (summed + bias_rows[None, None, None, :]).astype(jnp.bfloat16)
    image = image.reshape(members, windows * columns, own_rows)
    return jnp.transpose(image, (0, 2, 1))


def body(tokens, w_upper, w_surface, bias):
    lat_rows = tokens.shape[2]
    frames = project(tokens, w_upper, w_surface)
    return deliver(frames, bias, lat_rows)


def solution(mesh):
    placed = (P("grp", None, None, "win", None), P(), P(), P())
    return jax.shard_map(
        body, mesh=mesh, in_specs=placed, out_specs=P("grp", "win", None), check_vma=False
    )
```

profile of v0, /device:TPU:0, one launch (start us, length us, event | category | flops | bytes accessed | tf_op | source)
XLA Modules:
  0.0 201.6 jit_solution(15619941665332143231)
XLA Ops:
  0.0 0.0 copy-start
  0.0 1.3 copy.25
  1.3 0.1 reshape.46
  1.4 7.7 %convolution_bitcast_fusion = f32[2,3,2,4,5,7,2,2,4,64]{9,4,1,5,0,3,2,8,7,6:T(8,128)S(1)} fusion(bf16[2,8,64,3,384]{4,2,3,1,0:T(8,128)(2,1)} %param.4, bf16[384,5,2,2,4,2,4,1,1,1]{0,6,5,4,3,2,1,9,8,7:T(4,128)(2,1)S(1)} %bitcast.81), kind=kOutput, calls=%fused_computation.4 | convolution fusion | flops 1321205760 | bytes 9437184 | tf_op jit(solution)/shard_map/dvlpqrs,mzjdi->vlpqrsmzji/dot_general | solution.py:38
  9.1 8.7 %slice_bitcast_fusion.1 = (f32[2,3,4,5,7,2,2,4,64]{8,3,1,4,0,2,7,6,5:T(8,128)}, f32[2,3,4,5,7,2,2,4,64]{8,3,1,4,0,2,7,6,5:T(8,128)}) fusion(f32[2,3,2,4,5,7,2,2,4,64]{9,4,1,5,0,3,2,8,7,6:T(8,128)S(1)} %convolution_bitcast_fusion), kind=kLoop, calls=%fused_computation.3 | loop fusion | bytes 13762560 | tf_op jit(solution)/shard_map/squeeze | solution.py:13
  17.8 12.0 %fusion.1 = (f32[2,4,4,5,7,2,4,64]{7,3,1,4,0,2,6,5:T(8,128)S(1)}, f32[2,4,4,5,7,2,4,64]{7,3,1,4,0,2,6,5:T(8,128)}) fusion(f32[2,3,4,5,7,2,2,4,64]{8,3,1,4,0,2,7,6,5:T(8,128)} %get-tuple-element.7, f32[2,3,4,5,7,2,2,4,64]{8,3,1,4,0,2,7,6,5:T(8,128)} %get-tuple-element.8), kind=kLoop, calls=%fused_computation.6 | loop fusion | flops 1146880 | bytes 11468800 | tf_op jit(solution)/shard_map/squeeze | solution.py:23
  29.9 6.9 %fusion.3 = bf16[2,4,4,5,7,2,65,4]{6,3,1,4,0,2,7,5:T(8,128)(2,1)} fusion(f32[2,4,4,5,7,2,4,64]{7,3,1,4,0,2,6,5:T(8,128)} %get-tuple-element.6, f32[2,4,4,5,7,2,4,64]{7,3,1,4,0,2,6,5:T(8,128)S(1)} %get-tuple-element.5), kind=kLoop, calls=%fused_computation.10 | loop fusion | flops 1164800 | bytes 5752320 | tf_op jit(solution)/shard_map/transpose | solution.py:28
  36.7 31.0 %copy.29 = bf16[2,4,4,5,7,2,65,4]{7,6,2,1,5,4,3,0:T(8,128)(2,1)} copy(bf16[2,4,4,5,7,2,65,4]{6,3,1,4,0,2,7,5:T(8,128)(2,1)} %fusion.3) | data formatting | bytes 2329600 | tf_op jit(solution)/shard_map/transpose | solution.py:28
  67.7 0.0 copy-start.1
  67.7 39.4 %reshape.47 = bf16[2,16,5,14,260]{4,1,3,2,0:T(8,128)(2,1)S(1)} reshape(bf16[2,4,4,5,7,2,65,4]{7,6,2,1,5,4,3,0:T(8,128)(2,1)} %copy.29) | data formatting | bytes 2329600 | tf_op jit(solution)/shard_map/reshape | solution.py:44
  107.0 0.5 slice.84
  107.5 0.0 copy-done.1
  107.5 0.2 copy.30
  107.7 0.1 reshape.54
  107.8 1.4 convolution_bitcast_fusion.1
  109.2 0.1 slice_bitcast_fusion.3
  109.3 0.2 fusion.16
  109.5 0.9 fusion.20
  110.4 2.0 %copy.34 = bf16[2,4,4,4,65,4]{5,4,2,1,3,0:T(8,128)(2,1)S(1)} copy(bf16[2,4,4,4,65,4]{4,2,1,0,5,3:T(4,128)(2,1)} %fusion.20) | data formatting | bytes 133120 | tf_op jit(solution)/shard_map/transpose | solution.py:28
  112.4 1.3 reshape.50
  113.7 0.1 slice.89
  113.8 0.1 pad_maximum_fusion
  113.9 13.7 %copy.46 = bf16[2,16,69,256]{1,0,3,2:T(2,128)(2,1)} copy(bf16[2,16,69,256]{3,1,2,0:T(8,128)(2,1)S(1)} %pad_maximum_fusion) | data formatting | bytes 2260992 | tf_op jit(solution)/shard_map/convert_element_type | solution.py:57
  127.6 11.7 %reshape.60 = bf16[32,2,8832]{2,1,0:T(2,128)(2,1)} reshape(bf16[17664,2,16]{2,1,0:T(2,128)(2,1)} %bitcast.74) | data formatting | bytes 2260992
  139.4 7.3 %all-to-all-start = ((bf16[32,2,8832]{2,1,0:T(2,128)(2,1)}), bf16[32,2,8832]{2,1,0:T(2,128)(2,1)S(1)}, u32[]{:S(2)}, u32[]{:S(2)}) async-start(bf16[32,2,8832]{2,1,0:T(2,128)(2,1)} %reshape.60), calls=%async_computation | async-start | bytes 2260992 | tf_op jit(solution)/shard_map/all_to_all | solution.py:66
  146.7 0.0 copy-done
  146.7 0.3 convolution_reduce_fusion
  147.1 27.6 %all-to-all-done = bf16[32,2,8832]{2,1,0:T(2,128)(2,1)S(1)} async-done(((bf16[32,2,8832]{2,1,0:T(2,128)(2,1)}), bf16[32,2,8832]{2,1,0:T(2,128)(2,1)S(1)}, u32[]{:S(2)}, u32[]{:S(2)}) %all-to-all-start) | async-done | bytes 1130528 | tf_op jit(solution)/shard_map/all_to_all | solution.py:66
  174.7 8.2 %reshape.61 = bf16[17664,2,16]{2,1,0:T(2,128)(2,1)} reshape(bf16[32,2,8832]{2,1,0:T(2,128)(2,1)S(1)} %all-to-all-done) | data formatting | bytes 2260992
  182.9 14.4 %copy.47 = bf16[2,16,32,552]{3,2,1,0:T(8,128)(2,1)S(1)} copy(bf16[2,16,32,552]{1,0,3,2:T(2,128)(2,1)} %bitcast.75) | data formatting | bytes 2260992 | tf_op jit(solution)/shard_map/all_to_all | solution.py:66
  197.4 0.3 add_convert_fusion.1
  197.7 1.0 copy.38
  198.7 2.9 %copy.39 = bf16[2,552,384]{2,1,0:T(8,128)(2,1)} copy(bf16[2,552,384]{1,0,2:T(2,128)(2,1)S(1)} %bitcast.80) | data formatting | bytes 1695744 | tf_op jit(solution)/shard_map/transpose | solution.py:85
  (3 shorter events, 0.1 us)
Async XLA Ops:
  0.0 146.7 %copy-start = (f32[69]{0:T(128)S(1)}, f32[69]{0:T(128)}, u32[]{:S(2)}) copy-start(f32[69]{0:T(128)} %param.7) | copy-start | bytes 832
  67.7 39.8 %copy-start.1 = (bf16[384,256]{1,0:T(8,128)(2,1)S(1)}, bf16[384,256]{1,0:T(8,128)(2,1)}, u32[]{:S(2)}) copy-start(bf16[384,256]{1,0:T(8,128)(2,1)} %param.6) | copy-start | bytes 589828
  139.4 35.3 %all-to-all-start = ((bf16[32,2,8832]{2,1,0:T(2,128)(2,1)}), bf16[32,2,8832]{2,1,0:T(2,128)(2,1)S(1)}, u32[]{:S(2)}, u32[]{:S(2)}) async-start(bf16[32,2,8832]{2,1,0:T(2,128)(2,1)} %reshape.60), calls=%async_computation | async-start | bytes 2260992 | tf_op jit(solution)/shard_map/all_to_all | solution.py:66
where the time goes:
time: 204 us; the launch traced here: 202 us
  local copies, waits for them, and re-layouts  137 us (67%)
  waiting for transfers between devices  27.6 us (14%)
  other arithmetic  20.3 us (10%)
  matrix products  9.46 us (5%)
  starting transfers between devices  7.33 us (4%)
    reshape x1, local copies, waits for them, and re-layouts, project(): upper.reshape(members, frame_width, VARS_UP, 2 * upper_levels, (lat_rows...  39.4 us
    transpose x2, local copies, waits for them, and re-layouts, latitude_add(): return jnp.swapaxes(summed, -1, -2)  33 us
    all_to_all x1, waiting for transfers between devices, deliver(): lax.all_to_all(frames, 'win', split_axis=2, concat_axis=1, tiled=True)  27.6 us
    unnamed x8, local copies, waits for them, and re-layouts  21.4 us
    all_to_all x1, local copies, waits for them, and re-layouts, deliver(): lax.all_to_all(frames, 'win', split_axis=2, concat_axis=1, tiled=True)  14.4 us
    convert_element_type x1, local copies, waits for them, and re-layouts, project(): joined = jnp.concatenate([upper, surface], axis=2).astype(jnp.bfloat16)  13.7 us
    squeeze x2, other arithmetic, latitude_add(): first = values[..., 0, :, :]  12.2 us
    squeeze x2, local copies, waits for them, and re-layouts, intersection_add(): first = lax.index_in_dim(values, 0, axis + 1, keepdims=False)  8.84 us
  transfers between devices with their start and end apart: 1, of which 1 were waited for; matrix products, arithmetic and copies ran while one was open for 0% of the time, Pallas kernels for 0%

commit v1 on v0

--- a/solution.py
+++ b/solution.py
@@ -63,7 +63,10 @@
     members, frame_width, all_rows = frames.shape
     columns = frame_width - 2 * rim_width
     windows = lax.axis_size("win")
-    received = lax.all_to_all(frames, "win", split_axis=2, concat_axis=1, tiled=True)
+    received = jnp.concatenate(
+        lax.all_to_all(jnp.stack(jnp.split(frames, lax.axis_size("win"), axis=2)), "win", 0, 0),
+        axis=1,
+    )
     own_rows = received.shape[2]
     received = received.reshape(members, windows, frame_width, own_rows)
     inner = received[:, :, rim_width : frame_width - rim_width, :].astype(jnp.float32)

time: 204 us -> 185 us (0.907)
  local copies, waits for them, and re-layouts: 137 us -> 114 us
  waiting for transfers between devices: 27.6 us -> 31.6 us
    all_to_all x1 -> x0, local copies, waits for them, and re-layouts: 14.4 us -> none  [deliver(): lax.all_to_all(frames, 'win', split_axis=2, concat_axis=1, tiled=True)]
    convert_element_type x1, local copies, waits for them, and re-layouts: 13.7 us -> 0.65 us  [project(): joined = jnp.concatenate([upper, surface], axis=2).astype(jnp.bfloat16)]
    all_to_all x1, waiting for transfers between devices: 27.6 us -> 31.6 us  [deliver(): lax.all_to_all(jnp.stack(jnp.split(frames, lax.axis_size('win'), axis=2))...]
    unnamed x8 -> x37, local copies, waits for them, and re-layouts: 21.4 us -> 23.4 us
where the time goes in v1:
time: 185 us; the launch traced here: 183 us
  local copies, waits for them, and re-layouts  114 us (62%)
  waiting for transfers between devices  31.6 us (17%)
  other arithmetic  21.1 us (11%)
  matrix products  9.46 us (5%)
  starting transfers between devices  7.33 us (4%)
    reshape x1, local copies, waits for them, and re-layouts, project(): upper.reshape(members, frame_width, VARS_UP, 2 * upper_levels, (lat_rows...  39.3 us
    transpose x2, local copies, waits for them, and re-layouts, latitude_add(): return jnp.swapaxes(summed, -1, -2)  33 us
    all_to_all x1, waiting for transfers between devices, deliver(): lax.all_to_all(jnp.stack(jnp.split(frames, lax.axis_size('win'), axis=2))...  31.6 us
    unnamed x37, local copies, waits for them, and re-layouts  23.4 us
    squeeze x2, other arithmetic, latitude_add(): first = values[..., 0, :, :]  12.2 us
    squeeze x2, local copies, waits for them, and re-layouts, intersection_add(): first = lax.index_in_dim(values, 0, axis + 1, keepdims=False)  8.84 us
    transpose x2, other arithmetic, latitude_add(): return jnp.swapaxes(summed, -1, -2)  7.72 us
    dot_general x1, matrix products, project(): jnp.einsum('dvlpqrs,mzjdi->vlpqrsmzji', kernel_up, upper_tok, preferred_e...  7.67 us
  transfers between devices with their start and end apart: 1, of which 1 were waited for; matrix products, arithmetic and copies ran while one was open for 0% of the time, Pallas kernels for 0%

profile of v1, /device:TPU:0, one launch (start us, length us, event | category | flops | bytes accessed | tf_op | source)
XLA Modules:
  0.0 183.3 jit_solution(2037318045292900410)
XLA Ops:
  0.0 1.3 copy.56
  1.4 7.7 %convolution_bitcast_fusion = f32[2,3,2,4,5,7,2,2,4,64]{9,4,1,5,0,3,2,8,7,6:T(8,128)S(1)} fusion(bf16[2,8,64,3,384]{4,2,3,1,0:T(8,128)(2,1)} %param.4, bf16[384,5,2,2,4,2,4,1,1,1]{0,6,5,4,3,2,1,9,8,7:T(4,128)(2,1)S(1)} %bitcast.203), kind=kOutput, calls=%fused_computation.4 | convolution fusion | flops 1321205760 | bytes 9437184 | tf_op jit(solution)/shard_map/dvlpqrs,mzjdi->vlpqrsmzji/dot_general | solution.py:38
  9.1 8.7 %slice_bitcast_fusion.1 = (f32[2,3,4,5,7,2,2,4,64]{8,3,1,4,0,2,7,6,5:T(8,128)}, f32[2,3,4,5,7,2,2,4,64]{8,3,1,4,0,2,7,6,5:T(8,128)}) fusion(f32[2,3,2,4,5,7,2,2,4,64]{9,4,1,5,0,3,2,8,7,6:T(8,128)S(1)} %convolution_bitcast_fusion), kind=kLoop, calls=%fused_computation.3 | loop fusion | bytes 13762560 | tf_op jit(solution)/shard_map/squeeze | solution.py:13
  17.8 12.0 %fusion.1 = (f32[2,4,4,5,7,2,4,64]{7,3,1,4,0,2,6,5:T(8,128)S(1)}, f32[2,4,4,5,7,2,4,64]{7,3,1,4,0,2,6,5:T(8,128)}) fusion(f32[2,3,4,5,7,2,2,4,64]{8,3,1,4,0,2,7,6,5:T(8,128)} %get-tuple-element.7, f32[2,3,4,5,7,2,2,4,64]{8,3,1,4,0,2,7,6,5:T(8,128)} %get-tuple-element.8), kind=kLoop, calls=%fused_computation.6 | loop fusion | flops 1146880 | bytes 11468800 | tf_op jit(solution)/shard_map/squeeze | solution.py:23
  29.9 6.9 %fusion.3 = bf16[2,4,4,5,7,2,65,4]{6,3,1,4,0,2,7,5:T(8,128)(2,1)} fusion(f32[2,4,4,5,7,2,4,64]{7,3,1,4,0,2,6,5:T(8,128)} %get-tuple-element.6, f32[2,4,4,5,7,2,4,64]{7,3,1,4,0,2,6,5:T(8,128)S(1)} %get-tuple-element.5), kind=kLoop, calls=%fused_computation.10 | loop fusion | flops 1164800 | bytes 5752320 | tf_op jit(solution)/shard_map/transpose | solution.py:28
  36.7 31.0 %copy.60 = bf16[2,4,4,5,7,2,65,4]{7,6,2,1,5,4,3,0:T(8,128)(2,1)} copy(bf16[2,4,4,5,7,2,65,4]{6,3,1,4,0,2,7,5:T(8,128)(2,1)} %fusion.3) | data formatting | bytes 2329600 | tf_op jit(solution)/shard_map/transpose | solution.py:28
  67.7 39.3 %reshape.48 = bf16[2,16,5,14,260]{4,1,3,2,0:T(8,128)(2,1)S(1)} reshape(bf16[2,4,4,5,7,2,65,4]{7,6,2,1,5,4,3,0:T(8,128)(2,1)} %copy.60) | data formatting | bytes 2329600 | tf_op jit(solution)/shard_map/reshape | solution.py:44
  108.6 1.4 convolution_bitcast_fusion.1
  110.4 0.9 fusion.20
  111.3 2.0 %copy.65 = bf16[2,4,4,4,65,4]{5,4,2,1,3,0:T(8,128)(2,1)S(1)} copy(bf16[2,4,4,4,65,4]{4,2,1,0,5,3:T(4,128)(2,1)} %fusion.20) | data formatting | bytes 133120 | tf_op jit(solution)/shard_map/transpose | solution.py:28
  113.3 1.9 %reshape.51 = bf16[2,16,4,260]{3,1,2,0:T(8,128)(2,1)} reshape(bf16[2,4,4,4,65,4]{5,4,2,1,3,0:T(8,128)(2,1)S(1)} %copy.65) | data formatting | bytes 133120 | tf_op jit(solution)/shard_map/reshape | solution.py:55
  115.2 1.0 slice.89
  116.3 0.6 convert_element_type.34
  117.6 0.7 constant_dynamic-update-slice_fusion.30
  118.3 0.7 constant_dynamic-update-slice_fusion.29
  119.0 0.7 constant_dynamic-update-slice_fusion.28
  119.7 0.7 constant_dynamic-update-slice_fusion.27
  120.4 0.7 constant_dynamic-update-slice_fusion.26
  121.1 0.7 constant_dynamic-update-slice_fusion.25
  121.8 0.7 constant_dynamic-update-slice_fusion.24
  122.5 0.7 constant_dynamic-update-slice_fusion.23
  123.2 0.7 constant_dynamic-update-slice_fusion.22
  123.8 0.7 constant_dynamic-update-slice_fusion.21
  124.5 0.7 constant_dynamic-update-slice_fusion.20
  125.2 0.7 constant_dynamic-update-slice_fusion.19
  125.9 0.7 constant_dynamic-update-slice_fusion.18
  126.6 0.7 constant_dynamic-update-slice_fusion.17
  127.3 0.7 constant_dynamic-update-slice_fusion.16
  128.6 0.7 constant_dynamic-update-slice_fusion.14
  129.3 0.7 constant_dynamic-update-slice_fusion.13
  130.0 0.7 constant_dynamic-update-slice_fusion.12
  130.7 0.7 constant_dynamic-update-slice_fusion.11
  131.4 0.7 constant_dynamic-update-slice_fusion.10
  132.1 0.7 constant_dynamic-update-slice_fusion.9
  132.8 0.7 constant_dynamic-update-slice_fusion.8
  133.5 0.7 constant_dynamic-update-slice_fusion.7
  134.2 0.7 constant_dynamic-update-slice_fusion.6
  134.9 0.7 constant_dynamic-update-slice_fusion.5
  135.6 0.7 constant_dynamic-update-slice_fusion.4
  136.3 0.7 constant_dynamic-update-slice_fusion.3
  137.0 0.7 constant_dynamic-update-slice_fusion.2
  137.7 0.7 constant_dynamic-update-slice_fusion.1
  138.3 0.7 constant_dynamic-update-slice_fusion
  139.0 7.3 %all-to-all-start = ((bf16[32,2,16,552]{3,2,1,0:T(8,128)(2,1)}), bf16[32,2,16,552]{3,2,1,0:T(8,128)(2,1)S(1)}, u32[]{:S(2)}, u32[]{:S(2)}) async-start(bf16[32,2,16,552]{3,2,1,0:T(8,128)(2,1)} %constant_dynamic-update-slice_fusion), calls=%async_computation | async-start | bytes 2621440 | tf_op jit(solution)/shard_map/all_to_all | solution.py:67
  146.8 31.6 %all-to-all-done = bf16[32,2,16,552]{3,2,1,0:T(8,128)(2,1)S(1)} async-done(((bf16[32,2,16,552]{3,2,1,0:T(8,128)(2,1)}), bf16[32,2,16,552]{3,2,1,0:T(8,128)(2,1)S(1)}, u32[]{:S(2)}, u32[]{:S(2)}) %all-to-all-start) | async-done | bytes 1130528 | tf_op jit(solution)/shard_map/all_to_all | solution.py:67
  178.6 1.0 add_convert_fusion.1
  179.6 0.8 copy.68
  180.4 2.9 %copy.69 = bf16[2,552,384]{2,1,0:T(8,128)(2,1)} copy(bf16[2,552,384]{1,0,2:T(2,128)(2,1)S(1)} %bitcast.202) | data formatting | bytes 1695744 | tf_op jit(solution)/shard_map/transpose | solution.py:88
  (19 shorter events, 4.0 us)
Async XLA Ops:
  0.0 146.4 %copy-start = (f32[69]{0:T(128)S(1)}, f32[69]{0:T(128)}, u32[]{:S(2)}) copy-start(f32[69]{0:T(128)} %param.7) | copy-start | bytes 832
  107.5 0.9 copy-start.1
  139.0 39.3 %all-to-all-start = ((bf16[32,2,16,552]{3,2,1,0:T(8,128)(2,1)}), bf16[32,2,16,552]{3,2,1,0:T(8,128)(2,1)S(1)}, u32[]{:S(2)}, u32[]{:S(2)}) async-start(bf16[32,2,16,552]{3,2,1,0:T(8,128)(2,1)} %constant_dynamic-update-slice_fusion), calls=%async_computation | async-start | bytes 2621440 | tf_op jit(solution)/shard_map/all_to_all | solution.py:67
